TPU v7x, 64 devices: a 2x2x8 block of a 4x4x8 slice. The times are simulated.
64 devices in a mesh: dp: 8 (over x, y, core), tp: 8 (over z).
Axes of the slice: x: 2, y: 2, z: 8, core: 2. Of those that a mesh axis runs over, the one named last changes fastest.
The devices are a block of a 4x4x8 slice.
Arguments:
- x: bfloat16 [16384, 2048], P('dp'), parts along dimension 0
- dy: bfloat16 [16384, 2048], P('dp'), parts along dimension 0
- gate: bfloat16 [16384, 16384], P('dp', 'tp'), parts along dimension 0
- up: bfloat16 [16384, 16384], P('dp', 'tp'), parts along dimension 0
- w_gate: bfloat16 [2048, 16384], P(None, 'tp')
- w_up: bfloat16 [2048, 16384], P(None, 'tp')
- w_down: bfloat16 [16384, 2048], P('tp')
Outputs:
- output 1: bfloat16 [16384, 2048], P('dp'), parts along dimension 0
- output 2: bfloat16 [16384, 16384], P('dp', 'tp'), parts along dimension 0
- output 3: bfloat16 [16384, 16384], P('dp', 'tp'), parts along dimension 0
- output 4: bfloat16 [131072, 2048], P(('dp', 'tp')), parts along dimension 0
There are 8 independent parts. A program takes and returns all parts, laid end to end along the dimension named above; an argument that names none is the same for every part.
All inputs are finite; a program needn't handle non-finite values.
Results may differ from a plain program's by a relative error of at most 0.012.
Values are sent between devices in bfloat16 or wider.
A program may use at most 768 MiB of HBM per device.

v0:
```python
import functools

import jax
import jax.numpy as jnp
from jax import lax
from jax.experimental import pallas as pl
from jax.experimental.pallas import tpu as pltpu
from jax.sharding import PartitionSpec as P

BF, F32 = jnp.bfloat16, jnp.float32
NC = 4
MIB = 2**20


def nt(a, b):
    return lax.dot_general(a, b, (((1,), (1,)), ((), ())), preferred_element_type=F32)


def tn(a, b):
    return lax.dot_general(a, b, (((0,), (0,)), ((), ())), preferred_element_type=F32)


def gates(d_hidden, g, u):
    c, d = 0.7978845608028654, 0.044715
    g2 = g * g
    h = 0.5 * jnp.tanh(g * (c + (c * d) * g2)) + 0.5
    gelu = g * h
    slope = h + gelu * (1.0 - h) * (2.0 * c + (6.0 * c * d) * g2)
    return d_hidden * u * slope, d_hidden * gelu, gelu * u


def step_kernel(
    n, x, dy, gate, up, wg, wu, wd,
    dx, owg, owu, owd, kept,
    dyv, xv, gu, hb, hid,
    dy_sem, x_sem, gu_sem, kept_sem, hid_sem, w_sem, chunk_sem, send_sem, recv_sem,
):
    T, D = x.shape
    F = gate.shape[1]
    R = T // n
    H, FC, DC = R // 2, F // NC, D // NC
    me = lax.axis_index("tp")
    right, left = lax.rem(me + 1, n), lax.rem(me + n - 1, n)
    last = n - 1

    barrier = pltpu.get_barrier_semaphore()
    for peer in (left, right):
        pl.semaphore_signal(barrier, inc=1, device_id={"tp": peer})

    def rows_of(m):
        up_row = lax.rem(me + 3 * n - 1 - m, n) * R
        low_row = lax.rem(me + 1 + m, n) * R + H
        return pl.multiple_of(up_row, H), pl.multiple_of(low_row, H)

    def chunk(c, size):
        return pl.ds(pl.multiple_of(c * size, size), size)

    def load_rows(src, dst, k, sem):
        for half, row in enumerate(rows_of(k)):
            pltpu.make_async_copy(src.at[pl.ds(row, H), :], dst.at[pl.ds(pl.multiple_of(k * R + half * H, H), H), :], sem).start()

    def load_gu(k):
        slot = lax.rem(k, 2)
        for half, row in enumerate(rows_of(k)):
            for w, src in enumerate((gate, up)):
                for c in range(NC):
                    pltpu.make_async_copy(
                        src.at[pl.ds(row, H), pl.ds(c * FC, FC)],
                        gu.at[slot, pl.ds((w * NC + c) * R + half * H, H), :],
                        gu_sem.at[slot],
                    ).start()

    def wait(ref, sem):
        pltpu.make_async_copy(ref, ref, sem).wait()

    def load_w(src, dst, c, sem):
        return pltpu.make_async_copy(src.at[chunk(c, dst.shape[0] // NC), :], dst.at[chunk(c, dst.shape[0] // NC), :], sem)

    def message(m, c):
        copies = []
        for way, (row, peer) in enumerate(zip(rows_of(m), (right, left))):
            part = dx.at[pl.ds(row, H), chunk(c, DC)]
            copies.append(
                pltpu.make_async_remote_copy(
                    src_ref=part,
                    dst_ref=part,
                    send_sem=send_sem.at[way, c],
                    recv_sem=recv_sem.at[way, m, c],
                    device_id={"tp": peer},
                )
            )
        return copies

    def hidden(k, c):
        slot = lax.rem(k, 2)
        g_rows, u_rows = (pl.ds(pl.multiple_of((w * NC + c) * R, R), R) for w in range(2))
        d_hidden = nt(dyv[chunk(k, R), :], owd[chunk(c, FC), :])
        g, u = gu[slot, g_rows, :].astype(F32), gu[slot, u_rows, :].astype(F32)
        for buf, v in zip((hb.at[slot, 0], hb.at[slot, 1], hid), gates(d_hidden, g, u)):
            buf[:, chunk(c, FC)] = v.astype(BF)

    def keep(k, c):
        slot = lax.rem(k, 2)
        for w, buf in enumerate((hb.at[slot, 0], hb.at[slot, 1], hid)):
            pltpu.make_async_copy(
                buf.at[:, chunk(c, FC)],
                kept.at[w, c, chunk(k, R), :],
                hid_sem.at[c] if w == 2 else kept_sem.at[slot],
            ).start()

    def kept_hidden(c):
        wait(hid.at[:, chunk(c, FC)], hid_sem.at[c])

    def load_kept(q):
        w = lax.rem(q // NC + 2, 3)
        return pltpu.make_async_copy(kept.at[w, lax.rem(q, NC)], gu.at[lax.rem(q, 2)], chunk_sem.at[lax.rem(q, 2)])

    def load_step(k):
        load_rows(dy, dyv, k, dy_sem.at[k])
        load_gu(k)

    def loaded_step(k):
        wait(dyv.at[chunk(k, R), :], dy_sem.at[k])
        wait(gu.at[lax.rem(k, 2)], gu_sem.at[lax.rem(k, 2)])

    def term(k, c):
        slot = lax.rem(k, 2)
        return nt(hb[slot, 0], owg[chunk(c, DC), :]) + nt(hb[slot, 1], owu[chunk(c, DC), :])

    def arrived(m, c):
        for copy in message(m, c):
            copy.wait_recv()
            copy.wait_send()

    def send(m, c):
        for copy in message(m, c):
            copy.start()

    def add(k, c):
        acc = term(k, c)
        for half, row in enumerate(rows_of(k)):
            here = dx[pl.ds(row, H), chunk(c, DC)].astype(F32)
            dx[pl.ds(row, H), chunk(c, DC)] = (here + acc[half * H : (half + 1) * H, :]).astype(BF)

    down, gw, uw = (
        lambda c, w=w, src=src, dst=dst: load_w(src, dst, c, w_sem.at[w, c])
        for w, (src, dst) in enumerate(((wd, owd), (wg, owg), (wu, owu)))
    )
    load_rows(dy, dyv, 0, dy_sem.at[0])
    down(0).start()
    load_gu(0)
    down(1).start()
    loaded_step(0)
    for c in range(NC):
        down(c).wait()
        if c + 2 < NC:
            down(c + 2).start()
        elif c + 2 == NC:
            gw(0).start()
            uw(0).start()
        else:
            for b in range(1, NC):
                gw(b).start()
                uw(b).start()
            load_step(1)
        hidden(0, c)
        keep(0, c)
    pl.semaphore_wait(barrier, 2)

    def opening(c, _):
        @pl.when(c == 0)
        def _():
            loaded_step(1)
            load_step(2)

        gw(c).wait()
        uw(c).wait()
        kept_hidden(c)
        acc = term(0, c)
        for half, row in enumerate(rows_of(0)):
            dx[pl.ds(row, H), chunk(c, DC)] = acc[half * H : (half + 1) * H, :].astype(BF)
        send(0, c)
        hidden(1, c)
        keep(1, c)
        return 0

    lax.fori_loop(0, NC, opening, 0)
    load_rows(x, xv, 0, x_sem)

    def unit(i, _):
        k, c = i // NC, lax.rem(i, NC)

        @pl.when(c == 0)
        def _():
            loaded_step(k + 1)
            wait(hb.at[lax.rem(k + 1, 2)], kept_sem.at[lax.rem(k + 1, 2)])
            load_rows(x, xv, k, x_sem)

            @pl.when(k < last - 1)
            def _():
                load_step(k + 2)

        kept_hidden(c)
        arrived(k - 1, c)
        add(k, c)
        send(k, c)
        hidden(k + 1, c)
        keep(k + 1, c)
        return 0

    lax.fori_loop(NC, last * NC, unit, 0)
    load_rows(x, xv, last, x_sem)

    def closing(c, _):
        kept_hidden(c)
        arrived(last - 1, c)
        add(last, c)
        send(last, c)
        return 0

    lax.fori_loop(0, NC, closing, 0)
    for s in range(2):
        wait(hb.at[s], kept_sem.at[s])
    for s in range(2):
        load_kept(s).start()
    wait(xv, x_sem)

    def spread(i):
        m, c = n + i // NC, lax.rem(i, NC)
        arrived(m - 1, c)
        send(m, c)

    def grads(w):
        def body(j, _):
            i = w * 2 * NC + j
            q, half = i // 2, lax.rem(i, 2)
            c, slot = lax.rem(q, NC), lax.rem(q, 2)
            spread(i)

            @pl.when(half == 0)
            def _():
                load_kept(q).wait()

            side = chunk(half, D // 2)
            if w == 0:
                owd[chunk(c, FC), side] = tn(gu[slot], dyv[:, side]).astype(BF)
            else:
                (owg, owu)[w - 1][side, chunk(c, FC)] = tn(xv[:, side], gu[slot]).astype(BF)

            @pl.when(jnp.logical_and(half == 1, q < 3 * NC - 2))
            def _():
                load_kept(q + 2).start()

            return 0

        lax.fori_loop(0, 2 * NC, body, 0)

    for w in range(3):
        grads(w)
    for c in range(NC):
        arrived(2 * n - 3, c)


def store_kernel(*refs):
    count = len(refs) // 2
    sems = refs[-1]
    copies = [pltpu.make_async_copy(refs[i], refs[count + i], sems.at[i]) for i in range(count)]
    for copy in copies:
        copy.start()
    for copy in copies:
        copy.wait()


def solution(mesh):
    n = mesh.shape["tp"]

    def step(x, dy, gate, up, w_gate, w_up, w_down):
        T, D = x.shape
        F = gate.shape[1]
        R = T // n
        assert 2 * NC * R == T and (n - 2) * NC == 6 * NC
        shapes = [(T, D), (D, F), (D, F), (F, D)]
        hbm = pl.BlockSpec(memory_space=pl.ANY)
        vmem = pl.BlockSpec(memory_space=pltpu.VMEM)
        *outs, _ = pl.pallas_call(
            functools.partial(step_kernel, n),
            out_shape=[*(pltpu.VMEM(s, BF) for s in shapes), pltpu.HBM((3, NC, T, F // NC), BF)],
            in_specs=[hbm] * 7,
            out_specs=[vmem] * 4 + [hbm],
            scratch_shapes=[
                pltpu.VMEM((T, D), BF),
                pltpu.VMEM((T, D), BF),
                pltpu.VMEM((2, T, F // NC), BF),
                pltpu.VMEM((2, 2, R, F), BF),
                pltpu.VMEM((R, F), BF),
                pltpu.SemaphoreType.DMA((n,)),
                pltpu.SemaphoreType.DMA,
                pltpu.SemaphoreType.DMA((2,)),
                pltpu.SemaphoreType.DMA((2,)),
                pltpu.SemaphoreType.DMA((NC,)),
                pltpu.SemaphoreType.DMA((3, NC)),
                pltpu.SemaphoreType.DMA((2,)),
                pltpu.SemaphoreType.DMA((2, NC)),
                pltpu.SemaphoreType.DMA((2, 2 * n - 2, NC)),
            ],
            compiler_params=pltpu.CompilerParams(
                collective_id=0, has_side_effects=True, vmem_limit_bytes=30 * MIB
            ),
            name="mlp_backward",
        )(x, dy, gate, up, w_gate, w_up, w_down)
        store = lambda *o: pl.pallas_call(
            store_kernel,
            out_shape=[jax.ShapeDtypeStruct(s.shape, BF) for s in o],
            in_specs=[vmem] * len(o),
            out_specs=[hbm] * len(o),
            scratch_shapes=[pltpu.SemaphoreType.DMA((len(o),))],
            compiler_params=pltpu.CompilerParams(vmem_limit_bytes=1 * MIB),
            name="store",
        )(*o)
        dx, = store(outs[0])
        return dx, *store(*outs[1:])

    tokens, columns, rows = P("dp", None), P(None, "tp"), P("tp", None)
    return jax.shard_map(
        step,
        mesh=mesh,
        in_specs=(tokens, tokens, P("dp", "tp"), P("dp", "tp"), columns, columns, rows),
        out_specs=(tokens, P("dp", "tp"), P("dp", "tp"), P(("dp", "tp"), None)),
        check_vma=False,
    )
```

profile of v0, /device:TPU:21, one launch (start us, length us, event | category | flops | bytes accessed | tf_op | source)
XLA Modules:
  0.0 190.1 jit_solution(11928126759819645785)
XLA Ops:
  0.6 177.2 %mlp_backward.1 = (bf16[2048,2048]{1,0:T(8,128)(2,1)S(1)}, bf16[2048,2048]{1,0:T(8,128)(2,1)S(1)}, bf16[2048,2048]{1,0:T(8,128)(2,1)S(1)}, bf16[2048,2048]{1,0:T(8,128)(2,1)S(1)}, bf16[3,4,2048,512]{3,2,1,0:T(8,128)(2,1)}) custom-call(bf16[2048,2048]{1,0:T(8,128)(2,1)} %x.1, bf16[2048,2048]{1,0:T(8,128)(2,1)} %dy.1, bf16[2048,2048]{1,0:T(8,128)(2,1)} %gate.1, ...), custom_call_target="tpu_custom_call" | custom-call | tf_op jit(solution)/shard_map/mlp_backward/pallas_call | solution.py:285
  177.8 3.4 %store.2 = bf16[2048,2048]{1,0:T(8,128)(2,1)} custom-call(bf16[2048,2048]{1,0:T(8,128)(2,1)S(1)} %get-tuple-element.11.refs_0_), custom_call_target="tpu_custom_call" | custom-call | tf_op jit(solution)/shard_map/store/pallas_call | solution.py:311
  181.2 8.7 %store.3 = (bf16[2048,2048]{1,0:T(8,128)(2,1)}, bf16[2048,2048]{1,0:T(8,128)(2,1)}, bf16[2048,2048]{1,0:T(8,128)(2,1)}) custom-call(bf16[2048,2048]{1,0:T(8,128)(2,1)S(1)} %get-tuple-element.12.refs_0_, bf16[2048,2048]{1,0:T(8,128)(2,1)S(1)} %get-tuple-element.13.refs_1_, bf16[2048,2048]{1,0:T(8,128)(2,1)S(1)} %get-tuple-element.14.refs_2_), custom_call_target="tpu_custom_call" | custom-call | tf_op jit(solution)/shard_map/store/pallas_call | solution.py:311
where the time goes:
time: 190 us
  Pallas kernels  189 us (99%)
    pallas_call x1, Pallas kernels, step(): pl.pallas_call(functools.partial(step_kernel, n), out_shape=[*(pltpu.VMEM...  177 us
    pallas_call x2, Pallas kernels, step(): pl.pallas_call(store_kernel, out_shape=[jax.ShapeDtypeStruct(s.shape, BF)...  12.1 us

commit v1 on v0

--- a/solution.py
+++ b/solution.py
@@ -31,7 +31,7 @@
 
 def step_kernel(
     n, x, dy, gate, up, wg, wu, wd,
-    dx, owg, owu, owd, kept,
+    dx, owg, owu, owd, end_up, end_low, kept,
     dyv, xv, gu, hb, hid,
     dy_sem, x_sem, gu_sem, kept_sem, hid_sem, w_sem, chunk_sem, send_sem, recv_sem,
 ):
@@ -235,7 +235,9 @@
             i = w * 2 * NC + j
             q, half = i // 2, lax.rem(i, 2)
             c, slot = lax.rem(q, NC), lax.rem(q, 2)
-            spread(i)
+            @pl.when(i < (n - 3) * NC)
+            def _():
+                spread(i)
 
             @pl.when(half == 0)
             def _():
@@ -258,7 +260,9 @@
     for w in range(3):
         grads(w)
     for c in range(NC):
-        arrived(2 * n - 3, c)
+        arrived(2 * n - 4, c)
+        for end, row in zip((end_up, end_low), rows_of(2 * n - 3)):
+            end[:, pl.ds(c * DC, DC)] = dx[pl.ds(row, H), pl.ds(c * DC, DC)]
 
 
 def store_kernel(*refs):
@@ -271,6 +275,19 @@
         copy.wait()
 
 
+def merge_kernel(n, got_up, got_low, _, dx, sems):
+    H, me = got_up.shape[0], lax.axis_index("tp")
+    rows = lax.rem(me + 1, n) * 2 * H, lax.rem(me + n - 1, n) * 2 * H + H
+    copies = [
+        pltpu.make_async_copy(got, dx.at[pl.ds(pl.multiple_of(row, H), H), :], sems.at[i])
+        for i, (got, row) in enumerate(zip((got_up, got_low), rows))
+    ]
+    for copy in copies:
+        copy.start()
+    for copy in copies:
+        copy.wait()
+
+
 def solution(mesh):
     n = mesh.shape["tp"]
 
@@ -280,13 +297,14 @@
         R = T // n
         assert 2 * NC * R == T and (n - 2) * NC == 6 * NC
         shapes = [(T, D), (D, F), (D, F), (F, D)]
+        end = (R // 2, D)
         hbm = pl.BlockSpec(memory_space=pl.ANY)
         vmem = pl.BlockSpec(memory_space=pltpu.VMEM)
-        *outs, _ = pl.pallas_call(
+        *outs, end_up, end_low, _ = pl.pallas_call(
             functools.partial(step_kernel, n),
-            out_shape=[*(pltpu.VMEM(s, BF) for s in shapes), pltpu.HBM((3, NC, T, F // NC), BF)],
+            out_shape=[*(pltpu.VMEM(s, BF) for s in (*shapes, end, end)), pltpu.HBM((3, NC, T, F // NC), BF)],
             in_specs=[hbm] * 7,
-            out_specs=[vmem] * 4 + [hbm],
+            out_specs=[vmem] * 6 + [hbm],
             scratch_shapes=[
                 pltpu.VMEM((T, D), BF),
                 pltpu.VMEM((T, D), BF),
@@ -301,7 +319,7 @@
                 pltpu.SemaphoreType.DMA((3, NC)),
                 pltpu.SemaphoreType.DMA((2,)),
                 pltpu.SemaphoreType.DMA((2, NC)),
-                pltpu.SemaphoreType.DMA((2, 2 * n - 2, NC)),
+                pltpu.SemaphoreType.DMA((2, 2 * n - 3, NC)),
             ],
             compiler_params=pltpu.CompilerParams(
                 collective_id=0, has_side_effects=True, vmem_limit_bytes=30 * MIB
@@ -315,10 +333,24 @@
             out_specs=[hbm] * len(o),
             scratch_shapes=[pltpu.SemaphoreType.DMA((len(o),))],
             compiler_params=pltpu.CompilerParams(vmem_limit_bytes=1 * MIB),
+            cost_estimate=pl.CostEstimate(flops=2**31 * len(o), bytes_accessed=4 * T * D * len(o), transcendentals=0),
             name="store",
         )(*o)
-        dx, = store(outs[0])
-        return dx, *store(*outs[1:])
+        got_up = lax.ppermute(end_up, "tp", [(i, (i + 1) % n) for i in range(n)])
+        got_low = lax.ppermute(end_low, "tp", [(i, (i - 1) % n) for i in range(n)])
+        (dx,) = store(outs[0])
+        grads = store(*outs[1:])
+        dx = pl.pallas_call(
+            functools.partial(merge_kernel, n),
+            out_shape=jax.ShapeDtypeStruct(dx.shape, BF),
+            in_specs=[vmem, vmem, hbm],
+            out_specs=hbm,
+            scratch_shapes=[pltpu.SemaphoreType.DMA((2,))],
+            input_output_aliases={2: 0},
+            compiler_params=pltpu.CompilerParams(vmem_limit_bytes=2 * MIB),
+            name="merge",
+        )(got_up, got_low, dx)
+        return dx, *grads
 
     tokens, columns, rows = P("dp", None), P(None, "tp"), P("tp", None)
     return jax.shard_map(

time: 190 us -> 184 us (0.968)
  Pallas kernels: 189 us -> 180 us
  starting transfers between devices: 0 us -> 2.76 us
    pallas_call x1, Pallas kernels: 177 us -> 167 us  [step(): pl.pallas_call(functools.partial(step_kernel, n), out_shape=[*(pltpu.VMEM...]
    ppermute x0 -> x2, starting transfers between devices: none -> 2.76 us  [the longest x1 2.65 us: step(): got_low = lax.ppermute(end_low, 'tp', [(i, (i - 1) % n) for i in range(n)])]
  transfers between devices with their start and end apart: 0 -> 2, of which waited for: 0 -> 0; matrix products, arithmetic and copies ran while one was open for 0% -> 0% of each run, Pallas kernels for 0% -> 7%
where the time goes in v1:
time: 184 us; the launch traced here: 183 us
  Pallas kernels  180 us (98%)
  starting transfers between devices  2.76 us (2%)
    pallas_call x1, Pallas kernels, step(): pl.pallas_call(functools.partial(step_kernel, n), out_shape=[*(pltpu.VMEM...  167 us
    pallas_call x2, Pallas kernels, step(): pl.pallas_call(store_kernel, out_shape=[jax.ShapeDtypeStruct(s.shape, BF)...  12.1 us
  transfers between devices with their start and end apart: 2, of which 0 were waited for; matrix products, arithmetic and copies ran while one was open for 0% of the time, Pallas kernels for 7%

profile of v1, /device:TPU:21, one launch (start us, length us, event | category | flops | bytes accessed | tf_op | source)
XLA Modules:
  0.0 183.3 jit_solution(5170997483238005638)
XLA Ops:
  0.6 166.6 %mlp_backward.1 = (bf16[2048,2048]{1,0:T(8,128)(2,1)S(1)}, bf16[2048,2048]{1,0:T(8,128)(2,1)S(1)}, bf16[2048,2048]{1,0:T(8,128)(2,1)S(1)}, bf16[2048,2048]{1,0:T...) custom-call(bf16[2048,2048]{1,0:T(8,128)(2,1)} %x.1, ...), custom_call_target="tpu_custom_call" | custom-call | tf_op jit(solution)/shard_map/mlp_backward/pallas_call | solution.py:303
  167.3 0.1 collective-permute-start
  167.4 2.6 %collective-permute-start.1 = (bf16[128,2048]{1,0:T(8,128)(2,1)S(1)}, bf16[128,2048]{1,0:T(8,128)(2,1)S(1)}, u32[]{:S(2)}, u32[]{:S(2)}) collective-permute-start(bf16[128,2048]{1,0:T(8,128)(2,1)S(1)} %get-tuple-element.14), channel_id=1, source_target_pairs={{0,7},{1,0},{2,1},{3,2},{4,3},{5,4},{6,5},{7,6},{8,15},{9,8},{10,9... | collective-permute-start | bytes 1572872 | tf_op jit(solution)/shard_map/ppermute | solution.py:340
  170.0 3.4 %store.2._ = bf16[2048,2048]{1,0:T(8,128)(2,1)} custom-call(bf16[2048,2048]{1,0:T(8,128)(2,1)S(1)} %get-tuple-element.15.refs_0_), custom_call_target="tpu_custom_call" | custom-call | flops 2147483648 | bytes 16777216 | tf_op jit(solution)/shard_map/store/pallas_call | solution.py:329
  173.4 8.7 %store.3 = (bf16[2048,2048]{1,0:T(8,128)(2,1)}, bf16[2048,2048]{1,0:T(8,128)(2,1)}, bf16[2048,2048]{1,0:T(8,128)(2,1)}) custom-call(bf16[2048,2048]{1,0:T(8,128)(2,1)S(1)} %get-tuple-element.16.refs_0_, bf16[2048,2048]{1,0:T(8,128)(2,1)S(1)} %get-tuple-element.17.refs_1_, bf16[2048,2048]{1,0:T(8,128)(2,1)S(1)} %get-tuple-element.18.refs_2_), custom_call_target="tpu_custom_call" | custom-call | flops 6442450944 | bytes 50331648 | tf_op jit(solution)/shard_map/store/pallas_call | solution.py:329
  182.2 0.0 collective-permute-done.got_up
  182.2 0.0 collective-permute-done.1.got_low
  182.2 1.0 merge.1
Async XLA Ops:
  167.3 14.9 %collective-permute-start = (bf16[128,2048]{1,0:T(8,128)(2,1)S(1)}, bf16[128,2048]{1,0:T(8,128)(2,1)S(1)}, u32[]{:S(2)}, u32[]{:S(2)}) collective-permute-start(bf16[128,2048]{1,0:T(8,128)(2,1)S(1)} %get-tuple-element.13), channel_id=1, source_target_pairs={{0,1},{1,2},{2,3},{3,4},{4,5},{5,6},{6,7},{7,0},{8,9},{9,10},{10,1... | collective-permute-start | bytes 1572872 | tf_op jit(solution)/shard_map/ppermute | solution.py:339
  167.4 14.8 %collective-permute-start.1 = (bf16[128,2048]{1,0:T(8,128)(2,1)S(1)}, bf16[128,2048]{1,0:T(8,128)(2,1)S(1)}, u32[]{:S(2)}, u32[]{:S(2)}) collective-permute-start(bf16[128,2048]{1,0:T(8,128)(2,1)S(1)} %get-tuple-element.14), channel_id=1, source_target_pairs={{0,7},{1,0},{2,1},{3,2},{4,3},{5,4},{6,5},{7,6},{8,15},{9,8},{10,9... | collective-permute-start | bytes 1572872 | tf_op jit(solution)/shard_map/ppermute | solution.py:340
